TPU v7x, 32 devices: a whole 2x2x4 slice. The times are simulated.
32 devices in a mesh: row: 16 (over z, y, x), col: 2 (over core).
Axes of the slice: x: 2, y: 2, z: 4, core: 2. Of those that a mesh axis runs over, the one named last changes fastest.
Arguments:
- messages: float32 [32, 16, 2, 16, 128], P(('row', 'col')), may hold values from -6 to 6
- dst_local: int32 [32, 16, 2, 16], P(('row', 'col')), may hold values from 0 to 255
- counts: int32 [32, 16, 2], P(('row', 'col')), may hold values from 8 to 16, as said below
- degrees: int32 [8192], P(('row', 'col')), may hold values from 1 to 8
Outputs:
- aggregate: float32 [8192, 128], P(('row', 'col'))
Inputs may be any that keep to these rules, and one draw needn't show every extreme that they name: For every sender and group, the counts over the group's 2 ranges sum to exactly 24. In each group one range receives 16 live slots from every sender.
All inputs are finite; a program needn't handle non-finite values.
Results may differ from a plain program's by a relative error of at most 0.0003.
Values sent between devices are 32-bit elements; how exact they have to be, the bound alone decides.
No kernel may reach another device: no remote copies, remote signals or barrier semaphores. Data moves between devices by JAX's collectives and lax.ppermute only.
A program may use at most 64 MiB of HBM per device.

v0:
```python
import jax
import jax.numpy as jnp
from jax import lax
from jax.sharding import PartitionSpec as P


def body(messages, dst_local, counts, degrees):
    slots = messages.shape[3]
    width = messages.shape[4]
    owned = degrees.shape[0]
    slot_index = lax.broadcasted_iota(jnp.int32, counts.shape + (slots,), 3)
    alive_int = (slot_index < counts[..., None]).astype(jnp.int32)
    alive_mask = alive_int.astype(jnp.float32)
    masked = messages * alive_mask[..., None]
    received, labels = (
        lax.all_to_all(
            lax.all_to_all(masked, "row", split_axis=1, concat_axis=0, tiled=True),
            "col",
            split_axis=2,
            concat_axis=1,
            tiled=True,
        ),
        lax.all_to_all(
            lax.all_to_all(dst_local, "row", split_axis=1, concat_axis=0, tiled=True),
            "col",
            split_axis=2,
            concat_axis=1,
            tiled=True,
        ),
    )
    summed = jax.ops.segment_sum(
        received.reshape(-1, width), labels.reshape(-1), num_segments=owned
    )
    scale = jnp.maximum(degrees, 1).astype(jnp.float32)
    return summed / scale[:, None]


def solution(mesh):
    in_specs = (
        P(("row", "col"), None, None, None, None),
        P(("row", "col"), None, None, None),
        P(("row", "col"), None, None),
        P(("row", "col")),
    )
    out_specs = P(("row", "col"), None)
    return jax.shard_map(body, mesh=mesh, in_specs=in_specs, out_specs=out_specs, check_vma=False)
```

profile of v0, /device:TPU:0, one launch (start us, length us, event | category | flops | bytes accessed | tf_op | source)
XLA Modules:
  0.0 40.6 jit_solution(9112248974094976545)
XLA Ops:
  0.0 8.3 %all-to-all-start = ((s32[1,16,2,16]{3,2,0,1:T(2,128)}), s32[1,16,2,16]{3,2,0,1:T(2,128)S(1)}, u32[]{:S(2)}, u32[]{:S(2)}) async-start(s32[1,16,2,16]{3,2,0,1:T(2,128)} %bitcast.18), calls=%async_computation | async-start | bytes 32768 | tf_op jit(solution)/shard_map/all_to_all | solution.py:24
  8.3 0.0 copy-start
  8.4 0.7 %copy-done = s32[1,16,2]{1,2,0:T(2,128)S(1)} copy-done((s32[1,16,2]{1,2,0:T(2,128)S(1)}, s32[1,16,2]{1,2,0:T(2,128)}, u32[]{:S(2)}) %copy-start) | copy-done | bytes 152
  9.0 0.1 copy.15
  9.1 0.1 fusion.2
  9.2 1.8 %bitcast_multiply_fusion = f32[1,16,2,16,128]{4,3,2,0,1:T(8,128)} fusion(f32[1,16,2,16,128]{4,3,2,1,0:T(8,128)} %param.4, f32[16,2,16]{2,1,0:T(2,128)S(1)} %fusion.2), kind=kLoop, calls=%fused_computation.1 | loop fusion | flops 65536 | bytes 526336 | tf_op jit(solution)/shard_map/mul | solution.py:14
  11.0 4.7 %all-to-all-done = s32[1,16,2,16]{3,2,0,1:T(2,128)S(1)} async-done(((s32[1,16,2,16]{3,2,0,1:T(2,128)}), s32[1,16,2,16]{3,2,0,1:T(2,128)S(1)}, u32[]{:S(2)}, u32[]{:S(2)}) %all-to-all-start) | async-done | bytes 2080 | tf_op jit(solution)/shard_map/all_to_all | solution.py:24
  15.7 0.1 reshape.45
  15.8 3.7 %all_to_all.42 = s32[2,1,256]{2,1,0:T(1,128)S(1)} all-to-all(s32[2,1,256]{2,1,0:T(1,128)S(1)} %reshape.45), channel_id=1, replica_groups=mesh['row'=16,'col'=2] {'col'}, dimensions={0} | all-to-all | bytes 4096 | tf_op jit(solution)/shard_map/all_to_all | solution.py:23
  19.5 0.0 copy-start.1
  19.5 3.7 %all-to-all-start.2 = ((f32[1,16,2,16,128]{4,3,2,0,1:T(8,128)}), f32[1,16,2,16,128]{4,3,2,0,1:T(8,128)S(1)}, u32[]{:S(2)}, u32[]{:S(2)}) async-start(f32[1,16,2,16,128]{4,3,2,0,1:T(8,128)} %bitcast_multiply_fusion), calls=%async_computation.2 | async-start | bytes 524288 | tf_op jit(solution)/shard_map/all_to_all | solution.py:17
  23.1 0.0 copy-done.1
  23.2 0.5 %broadcast.9 = s32[]{:T(128)} broadcast(s32[]{:T(128)} %constant.8), dimensions={} | broadcast | bytes 8 | tf_op jit(solution)/shard_map/all_to_all | solution.py:23
  23.7 0.7 %reduce = s32[2,256]{1,0:T(2,128)S(1)} reduce(s32[2,1,256]{2,1,0:T(1,128)S(1)} %all_to_all.42, s32[]{:T(128)} %broadcast.9), dimensions={1}, to_apply=%all_to_all.14.reduce_sub_computation | reduce | bytes 4100 | tf_op jit(solution)/shard_map/all_to_all | solution.py:23
  24.3 0.1 reshape.46
  24.4 0.1 reshape.36
  24.5 9.0 %all-to-all-done.2 = f32[1,16,2,16,128]{4,3,2,0,1:T(8,128)S(1)} async-done(((f32[1,16,2,16,128]{4,3,2,0,1:T(8,128)}), f32[1,16,2,16,128]{4,3,2,0,1:T(8,128)S(1)}, u32[]{:S(2)}, u32[]{:S(2)}) %all-to-all-start.2) | async-done | bytes 262176 | tf_op jit(solution)/shard_map/all_to_all | solution.py:17
  33.6 3.9 %all_to_all.43 = f32[16,1,2,16,128]{4,3,0,1,2:T(8,128)S(1)} all-to-all(f32[16,1,2,16,128]{4,3,0,1,2:T(8,128)S(1)} %copy.17), channel_id=1, replica_groups=mesh['row'=16,'col'=2] {'col'}, dimensions={2} | all-to-all | bytes 524288 | tf_op jit(solution)/shard_map/all_to_all | solution.py:16
  37.5 2.3 %scatter_custom_fusion = f32[256,128]{1,0:T(8,128)S(1)} fusion(s32[512]{0:T(512)S(1)} %reshape.36, f32[512,128]{1,0:T(8,128)S(1)} %bitcast.14, f32[]{:T(128)} %constant.0.clone.1), kind=kCustom, calls=%fused_computation.3 | custom fusion | flops 65536 | bytes 131076 | tf_op jit(solution)/shard_map/scatter-add | solution.py:31
  39.8 0.8 %broadcast_divide_fusion = f32[256,128]{1,0:T(8,128)} fusion(f32[256,128]{1,0:T(8,128)S(1)} %scatter_custom_fusion, f32[256]{0:T(256)S(1)} %maximum_convert_fusion), kind=kLoop, calls=%fused_computation.2 | loop fusion | flops 32768 | bytes 263168 | tf_op jit(solution)/shard_map/div | solution.py:35
  (5 shorter events, 0.1 us)
Async XLA Ops:
  0.0 15.7 %all-to-all-start = ((s32[1,16,2,16]{3,2,0,1:T(2,128)}), s32[1,16,2,16]{3,2,0,1:T(2,128)S(1)}, u32[]{:S(2)}, u32[]{:S(2)}) async-start(s32[1,16,2,16]{3,2,0,1:T(2,128)} %bitcast.18), calls=%async_computation | async-start | bytes 32768 | tf_op jit(solution)/shard_map/all_to_all | solution.py:24
  8.3 0.7 %copy-start = (s32[1,16,2]{1,2,0:T(2,128)S(1)}, s32[1,16,2]{1,2,0:T(2,128)}, u32[]{:S(2)}) copy-start(s32[1,16,2]{1,2,0:T(2,128)} %param.6) | copy-start | bytes 388
  19.5 3.7 %copy-start.1 = (s32[256]{0:T(256)S(1)}, s32[256]{0:T(256)}, u32[]{:S(2)}) copy-start(s32[256]{0:T(256)} %param.7) | copy-start | bytes 3076
  19.5 14.1 %all-to-all-start.2 = ((f32[1,16,2,16,128]{4,3,2,0,1:T(8,128)}), f32[1,16,2,16,128]{4,3,2,0,1:T(8,128)S(1)}, u32[]{:S(2)}, u32[]{:S(2)}) async-start(f32[1,16,2,16,128]{4,3,2,0,1:T(8,128)} %bitcast_multiply_fusion), calls=%async_computation.2 | async-start | bytes 524288 | tf_op jit(solution)/shard_map/all_to_all | solution.py:17
where the time goes:
time: 41 us; the launch traced here: 40.6 us
  waiting for transfers between devices  13.7 us (33%)
  starting transfers between devices  12 us (29%)
  blocking collectives  7.63 us (19%)
  other arithmetic  5.57 us (14%)
  local copies, waits for them, and re-layouts  1.57 us (4%)
    all_to_all x1, waiting for transfers between devices, body(): lax.all_to_all(masked, 'row', split_axis=1, concat_axis=0, tiled=True)  9.04 us
    all_to_all x1, starting transfers between devices, body(): lax.all_to_all(dst_local, 'row', split_axis=1, concat_axis=0, tiled=True)  8.34 us
    all_to_all x1, waiting for transfers between devices, body(): lax.all_to_all(dst_local, 'row', split_axis=1, concat_axis=0, tiled=True)  4.7 us
    all_to_all x1, blocking collectives, body(): lax.all_to_all(lax.all_to_all(masked, 'row', split_axis=1, concat_axis=0,...  3.94 us
    all_to_all x1, blocking collectives, body(): lax.all_to_all(lax.all_to_all(dst_local, 'row', split_axis=1, concat_axis...  3.69 us
    all_to_all x1, starting transfers between devices, body(): lax.all_to_all(masked, 'row', split_axis=1, concat_axis=0, tiled=True)  3.66 us
    scatter-add x1, other arithmetic, body(): jax.ops.segment_sum(received.reshape(-1, width), labels.reshape(-1), num_...  2.28 us
    mul x1, other arithmetic, body(): masked = messages * alive_mask[..., None]  1.78 us
  transfers between devices with their start and end apart: 2, of which 2 were waited for; matrix products, arithmetic and copies ran while one was open for 8% of the time, Pallas kernels for 0%

commit v1 on v0

--- a/solution.py
+++ b/solution.py
@@ -2,6 +2,28 @@
 import jax.numpy as jnp
 from jax import lax
 from jax.sharding import PartitionSpec as P
+
+
+def cut_along(x, dim, size):
+    before, after = (x.shape[:dim], x.shape[dim + 1 :])
+    return jnp.moveaxis(x.reshape(*before, size, -1, *after), dim, 0)
+
+
+def laid_out(parts, dim):
+    parts = jnp.moveaxis(parts, 0, dim)
+    lengths = parts.shape
+    return parts.reshape(*lengths[:dim], lengths[dim] * lengths[dim + 1], *lengths[dim + 2 :])
+
+
+def exchange_in_pairs(shard, axis, split_dim, concat_dim):
+    size, index = (lax.axis_size(axis), lax.axis_index(axis))
+    parts = cut_along(shard, split_dim, size)
+    gathered = [parts[index]]
+    for step in range(1, size):
+        sent = parts[index ^ step]
+        gathered.append(lax.ppermute(sent, axis, [(i, i ^ step) for i in range(size)]))
+    parts = jnp.stack(gathered)[index ^ jnp.arange(size)]
+    return laid_out(parts, concat_dim)
 
 
 def body(messages, dst_local, counts, degrees):
@@ -21,7 +43,7 @@
             tiled=True,
         ),
         lax.all_to_all(
-            lax.all_to_all(dst_local, "row", split_axis=1, concat_axis=0, tiled=True),
+            exchange_in_pairs(dst_local, "row", 1, 0),
             "col",
             split_axis=2,
             concat_axis=1,

time: 41 us -> 64.5 us (1.57)
  starting transfers between devices: 12 us -> 31.6 us
  waiting for transfers between devices: 13.7 us -> 16.1 us
  local copies, waits for them, and re-layouts: 1.57 us -> 3.01 us
    ppermute x0 -> x15, starting transfers between devices: none -> 27.9 us  [exchange_in_pairs(): lax.ppermute(sent, axis, [(i, i ^ step) for i in range(size)])]
    all_to_all x1 -> x0, starting transfers between devices: 8.34 us -> none  [body(): lax.all_to_all(dst_local, 'row', split_axis=1, concat_axis=0, tiled=True)]
    ppermute x0 -> x15, waiting for transfers between devices: none -> 7.09 us  [exchange_in_pairs(): lax.ppermute(sent, axis, [(i, i ^ step) for i in range(size)])]
    all_to_all x1 -> x0, waiting for transfers between devices: 4.7 us -> none  [body(): lax.all_to_all(dst_local, 'row', split_axis=1, concat_axis=0, tiled=True)]
    unnamed x6 -> x23, local copies, waits for them, and re-layouts: 0.84 us -> 1.66 us
  transfers between devices with their start and end apart: 2 -> 16, of which waited for: 2 -> 4; matrix products, arithmetic and copies ran while one was open for 8% -> 5% of each run, Pallas kernels for 0% -> 0%
where the time goes in v1:
time: 64.5 us; the launch traced here: 64 us
  starting transfers between devices  31.6 us (49%)
  waiting for transfers between devices  16.1 us (25%)
  blocking collectives  7.63 us (12%)
  other arithmetic  5.6 us (9%)
  local copies, waits for them, and re-layouts  3.01 us (5%)
    ppermute x15, starting transfers between devices, exchange_in_pairs(): lax.ppermute(sent, axis, [(i, i ^ step) for i in range(size)])  27.9 us
    all_to_all x1, waiting for transfers between devices, body(): lax.all_to_all(masked, 'row', split_axis=1, concat_axis=0, tiled=True)  9.04 us
    ppermute x15, waiting for transfers between devices, exchange_in_pairs(): lax.ppermute(sent, axis, [(i, i ^ step) for i in range(size)])  7.09 us
    all_to_all x1, blocking collectives, body(): lax.all_to_all(lax.all_to_all(masked, 'row', split_axis=1, concat_axis=0,...  3.94 us
    all_to_all x1, blocking collectives, body(): lax.all_to_all(exchange_in_pairs(dst_local, 'row', 1, 0), 'col', split_ax...  3.69 us
    all_to_all x1, starting transfers between devices, body(): lax.all_to_all(masked, 'row', split_axis=1, concat_axis=0, tiled=True)  3.66 us
    scatter-add x1, other arithmetic, body(): jax.ops.segment_sum(received.reshape(-1, width), labels.reshape(-1), num_...  2.28 us
    mul x1, other arithmetic, body(): masked = messages * alive_mask[..., None]  1.79 us
  transfers between devices with their start and end apart: 16, of which 4 were waited for; matrix products, arithmetic and copies ran while one was open for 5% of the time, Pallas kernels for 0%

profile of v1, /device:TPU:0, one launch (start us, length us, event | category | flops | bytes accessed | tf_op | source)
XLA Modules:
  0.0 64.0 jit_solution(13253510728716210842)
XLA Ops:
  0.0 0.7 %copy-done = s32[1,16,2,16]{3,2,1,0:T(2,128)S(1)} copy-done((s32[1,16,2,16]{3,2,1,0:T(2,128)S(1)}, s32[1,16,2,16]{3,2,1,0:T(2,128)}, u32[]{:S(2)}) %copy-start) | copy-done | bytes 2072
  0.7 3.0 %collective-permute-start = (s32[1,1,2,16]{3,2,1,0:T(2,128)S(1)}, s32[1,1,2,16]{3,2,1,0:T(2,128)S(1)}, u32[]{:S(2)}, u32[]{:S(2)}) collective-permute-start(s32[1,1,2,16]{3,2,1,0:T(2,128)S(1)} %get-tuple-element.18), channel_id=1, source_target_pairs={{0,2},{2,0},{4,6},{6,4},{8,10},{10,8},{12,14},{14,12},{16,18},{18,... | collective-permute-start | bytes 392 | tf_op jit(solution)/shard_map/ppermute | solution.py:24
  3.8 1.5 %collective-permute-start.1 = (s32[1,1,2,16]{3,2,1,0:T(2,128)S(1)}, s32[1,1,2,16]{3,2,1,0:T(2,128)S(1)}, u32[]{:S(2)}, u32[]{:S(2)}) collective-permute-start(s32[1,1,2,16]{3,2,1,0:T(2,128)S(1)} %get-tuple-element.17), channel_id=1, source_target_pairs={{0,4},{2,6},{4,0},{6,2},{8,12},{10,14},{12,8},{14,10},{16,20},{18,... | collective-permute-start | bytes 392 | tf_op jit(solution)/shard_map/ppermute | solution.py:24
  5.3 2.0 %collective-permute-start.3 = (s32[1,1,2,16]{3,2,1,0:T(2,128)S(1)}, s32[1,1,2,16]{3,2,1,0:T(2,128)S(1)}, u32[]{:S(2)}, u32[]{:S(2)}) collective-permute-start(s32[1,1,2,16]{3,2,1,0:T(2,128)S(1)} %get-tuple-element.15), channel_id=1, source_target_pairs={{0,8},{2,10},{4,12},{6,14},{8,0},{10,2},{12,4},{14,6},{16,24},{18,... | collective-permute-start | bytes 392 | tf_op jit(solution)/shard_map/ppermute | solution.py:24
  7.3 1.4 %collective-permute-start.4 = (s32[1,1,2,16]{3,2,1,0:T(2,128)S(1)}, s32[1,1,2,16]{3,2,1,0:T(2,128)S(1)}, u32[]{:S(2)}, u32[]{:S(2)}) collective-permute-start(s32[1,1,2,16]{3,2,1,0:T(2,128)S(1)} %get-tuple-element.14), channel_id=1, source_target_pairs={{0,10},{2,8},{4,14},{6,12},{8,2},{10,0},{12,6},{14,4},{16,26},{18,... | collective-permute-start | bytes 392 | tf_op jit(solution)/shard_map/ppermute | solution.py:24
  8.7 0.7 %copy-done.1 = s32[1,16,2]{1,2,0:T(2,128)S(1)} copy-done((s32[1,16,2]{1,2,0:T(2,128)S(1)}, s32[1,16,2]{1,2,0:T(2,128)}, u32[]{:S(2)}) %copy-start.1) | copy-done | bytes 152
  9.4 0.1 copy.13
  9.5 0.1 fusion.2
  9.6 1.8 %bitcast_multiply_fusion = f32[1,16,2,16,128]{4,3,2,0,1:T(8,128)} fusion(f32[1,16,2,16,128]{4,3,2,1,0:T(8,128)} %param.4, f32[16,2,16]{2,1,0:T(2,128)S(1)} %fusion.2), kind=kLoop, calls=%fused_computation.2 | loop fusion | flops 65536 | bytes 526336 | tf_op jit(solution)/shard_map/mul | solution.py:36
  11.4 2.5 %collective-permute-start.5 = (s32[1,1,2,16]{3,2,1,0:T(2,128)S(1)}, s32[1,1,2,16]{3,2,1,0:T(2,128)S(1)}, u32[]{:S(2)}, u32[]{:S(2)}) collective-permute-start(s32[1,1,2,16]{3,2,1,0:T(2,128)S(1)} %get-tuple-element.13), channel_id=1, source_target_pairs={{0,12},{2,14},{4,8},{6,10},{8,4},{10,6},{12,0},{14,2},{16,28},{18,... | collective-permute-start | bytes 392 | tf_op jit(solution)/shard_map/ppermute | solution.py:24
  14.0 2.9 %collective-permute-start.7 = (s32[1,1,2,16]{3,2,1,0:T(2,128)S(1)}, s32[1,1,2,16]{3,2,1,0:T(2,128)S(1)}, u32[]{:S(2)}, u32[]{:S(2)}) collective-permute-start(s32[1,1,2,16]{3,2,1,0:T(2,128)S(1)} %get-tuple-element.11), channel_id=1, source_target_pairs={{0,16},{2,18},{4,20},{6,22},{8,24},{10,26},{12,28},{14,30},{16,0},... | collective-permute-start | bytes 392 | tf_op jit(solution)/shard_map/ppermute | solution.py:24
  16.9 1.3 %collective-permute-start.8 = (s32[1,1,2,16]{3,2,1,0:T(2,128)S(1)}, s32[1,1,2,16]{3,2,1,0:T(2,128)S(1)}, u32[]{:S(2)}, u32[]{:S(2)}) collective-permute-start(s32[1,1,2,16]{3,2,1,0:T(2,128)S(1)} %get-tuple-element.10), channel_id=1, source_target_pairs={{0,18},{2,16},{4,22},{6,20},{8,26},{10,24},{12,30},{14,28},{16,2},... | collective-permute-start | bytes 392 | tf_op jit(solution)/shard_map/ppermute | solution.py:24
  18.2 3.5 %collective-permute-start.9 = (s32[1,1,2,16]{3,2,1,0:T(2,128)S(1)}, s32[1,1,2,16]{3,2,1,0:T(2,128)S(1)}, u32[]{:S(2)}, u32[]{:S(2)}) collective-permute-start(s32[1,1,2,16]{3,2,1,0:T(2,128)S(1)} %get-tuple-element.9), channel_id=1, source_target_pairs={{0,20},{2,22},{4,16},{6,18},{8,28},{10,30},{12,24},{14,26},{16,4},... | collective-permute-start | bytes 392 | tf_op jit(solution)/shard_map/ppermute | solution.py:24
  21.7 0.1 collective-permute-start.10
  21.8 3.8 %collective-permute-start.11 = (s32[1,1,2,16]{3,2,1,0:T(2,128)S(1)}, s32[1,1,2,16]{3,2,1,0:T(2,128)S(1)}, u32[]{:S(2)}, u32[]{:S(2)}) collective-permute-start(s32[1,1,2,16]{3,2,1,0:T(2,128)S(1)} %get-tuple-element.7), channel_id=1, source_target_pairs={{0,24},{2,26},{4,28},{6,30},{8,16},{10,18},{12,20},{14,22},{16,8},... | collective-permute-start | bytes 392 | tf_op jit(solution)/shard_map/ppermute | solution.py:24
  25.6 1.2 %collective-permute-start.12 = (s32[1,1,2,16]{3,2,1,0:T(2,128)S(1)}, s32[1,1,2,16]{3,2,1,0:T(2,128)S(1)}, u32[]{:S(2)}, u32[]{:S(2)}) collective-permute-start(s32[1,1,2,16]{3,2,1,0:T(2,128)S(1)} %get-tuple-element.6), channel_id=1, source_target_pairs={{0,26},{2,24},{4,30},{6,28},{8,18},{10,16},{12,22},{14,20},{16,10}... | collective-permute-start | bytes 392 | tf_op jit(solution)/shard_map/ppermute | solution.py:24
  26.8 4.6 %collective-permute-start.13 = (s32[1,1,2,16]{3,2,1,0:T(2,128)S(1)}, s32[1,1,2,16]{3,2,1,0:T(2,128)S(1)}, u32[]{:S(2)}, u32[]{:S(2)}) collective-permute-start(s32[1,1,2,16]{3,2,1,0:T(2,128)S(1)} %get-tuple-element.19), channel_id=1, source_target_pairs={{0,28},{2,30},{4,24},{6,26},{8,20},{10,22},{12,16},{14,18},{16,12}... | collective-permute-start | bytes 392 | tf_op jit(solution)/shard_map/ppermute | solution.py:24
  31.4 0.4 collective-permute-done.12
  31.9 1.2 %collective-permute-done.13 = s32[1,1,2,16]{3,2,1,0:T(2,128)S(1)} collective-permute-done((s32[1,1,2,16]{3,2,1,0:T(2,128)S(1)}, s32[1,1,2,16]{3,2,1,0:T(2,128)S(1)}, u32[]{:S(2)}, u32[]{:S(2)}) %collective-permute-start.13) | collective-permute-done | bytes 160 | tf_op jit(solution)/shard_map/ppermute | solution.py:24
  33.1 5.5 %collective-permute-done.14 = s32[1,1,2,16]{3,2,1,0:T(2,128)S(1)} collective-permute-done((s32[1,1,2,16]{3,2,1,0:T(2,128)S(1)}, s32[1,1,2,16]{3,2,1,0:T(2,128)S(1)}, u32[]{:S(2)}, u32[]{:S(2)}) %collective-permute-start.14) | collective-permute-done | bytes 160 | tf_op jit(solution)/shard_map/ppermute | solution.py:24
  38.5 0.6 gather_fusion
  39.1 0.1 reshape.108
  39.2 3.7 %all_to_all.30 = s32[2,1,256]{2,1,0:T(1,128)S(1)} all-to-all(s32[2,1,256]{2,1,0:T(1,128)S(1)} %reshape.108), channel_id=1, replica_groups=mesh['row'=16,'col'=2] {'col'}, dimensions={0} | all-to-all | bytes 4096 | tf_op jit(solution)/shard_map/all_to_all | solution.py:45
  42.9 3.7 %all-to-all-start.1 = ((f32[1,16,2,16,128]{4,3,2,0,1:T(8,128)}), f32[1,16,2,16,128]{4,3,2,0,1:T(8,128)S(1)}, u32[]{:S(2)}, u32[]{:S(2)}) async-start(f32[1,16,2,16,128]{4,3,2,0,1:T(8,128)} %bitcast_multiply_fusion), calls=%async_computation.1 | async-start | bytes 524288 | tf_op jit(solution)/shard_map/all_to_all | solution.py:39
  46.6 0.5 broadcast.44
  47.1 0.7 %reduce = s32[2,256]{1,0:T(2,128)S(1)} reduce(s32[2,1,256]{2,1,0:T(1,128)S(1)} %all_to_all.30, s32[]{:T(128)} %broadcast.44), dimensions={1}, to_apply=%all_to_all.8.reduce_sub_computation | reduce | bytes 4100 | tf_op jit(solution)/shard_map/all_to_all | solution.py:45
  47.8 0.1 reshape.109
  47.9 0.1 reshape.96
  47.9 9.0 %all-to-all-done.1 = f32[1,16,2,16,128]{4,3,2,0,1:T(8,128)S(1)} async-done(((f32[1,16,2,16,128]{4,3,2,0,1:T(8,128)}), f32[1,16,2,16,128]{4,3,2,0,1:T(8,128)S(1)}, u32[]{:S(2)}, u32[]{:S(2)}) %all-to-all-start.1) | async-done | bytes 262176 | tf_op jit(solution)/shard_map/all_to_all | solution.py:39
  57.0 3.9 %all_to_all.31 = f32[16,1,2,16,128]{4,3,0,1,2:T(8,128)S(1)} all-to-all(f32[16,1,2,16,128]{4,3,0,1,2:T(8,128)S(1)} %copy.15), channel_id=1, replica_groups=mesh['row'=16,'col'=2] {'col'}, dimensions={2} | all-to-all | bytes 524288 | tf_op jit(solution)/shard_map/all_to_all | solution.py:38
  61.0 2.3 %scatter_custom_fusion = f32[256,128]{1,0:T(8,128)S(1)} fusion(s32[512]{0:T(512)S(1)} %reshape.96, f32[512,128]{1,0:T(8,128)S(1)} %bitcast.50, f32[]{:T(128)} %constant.20.clone.1), kind=kCustom, calls=%fused_computation.4 | custom fusion | flops 65536 | bytes 131076 | tf_op jit(solution)/shard_map/scatter-add | solution.py:53
  63.3 0.8 %broadcast_divide_fusion = f32[256,128]{1,0:T(8,128)} fusion(f32[256,128]{1,0:T(8,128)S(1)} %scatter_custom_fusion, f32[256]{0:T(256)S(1)} %maximum_convert_fusion), kind=kLoop, calls=%fused_computation.3 | loop fusion | flops 32768 | bytes 263168 | tf_op jit(solution)/shard_map/div | solution.py:57
  (43 shorter events, 0.4 us)
Async XLA Ops:
  0.0 0.7 %copy-start = (s32[1,16,2,16]{3,2,1,0:T(2,128)S(1)}, s32[1,16,2,16]{3,2,1,0:T(2,128)}, u32[]{:S(2)}) copy-start(s32[1,16,2,16]{3,2,1,0:T(2,128)} %param.5) | copy-start | bytes 6148
  0.7 10.6 %collective-permute-start = (s32[1,1,2,16]{3,2,1,0:T(2,128)S(1)}, s32[1,1,2,16]{3,2,1,0:T(2,128)S(1)}, u32[]{:S(2)}, u32[]{:S(2)}) collective-permute-start(s32[1,1,2,16]{3,2,1,0:T(2,128)S(1)} %get-tuple-element.18), channel_id=1, source_target_pairs={{0,2},{2,0},{4,6},{6,4},{8,10},{10,8},{12,14},{14,12},{16,18},{18,... | collective-permute-start | bytes 392 | tf_op jit(solution)/shard_map/ppermute | solution.py:24
  3.8 10.2 %collective-permute-start.1 = (s32[1,1,2,16]{3,2,1,0:T(2,128)S(1)}, s32[1,1,2,16]{3,2,1,0:T(2,128)S(1)}, u32[]{:S(2)}, u32[]{:S(2)}) collective-permute-start(s32[1,1,2,16]{3,2,1,0:T(2,128)S(1)} %get-tuple-element.17), channel_id=1, source_target_pairs={{0,4},{2,6},{4,0},{6,2},{8,12},{10,14},{12,8},{14,10},{16,20},{18,... | collective-permute-start | bytes 392 | tf_op jit(solution)/shard_map/ppermute | solution.py:24
  5.3 8.7 %collective-permute-start.2 = (s32[1,1,2,16]{3,2,1,0:T(2,128)S(1)}, s32[1,1,2,16]{3,2,1,0:T(2,128)S(1)}, u32[]{:S(2)}, u32[]{:S(2)}) collective-permute-start(s32[1,1,2,16]{3,2,1,0:T(2,128)S(1)} %get-tuple-element.16), channel_id=1, source_target_pairs={{0,6},{2,4},{4,2},{6,0},{8,14},{10,12},{12,10},{14,8},{16,22},{18,... | collective-permute-start | bytes 392 | tf_op jit(solution)/shard_map/ppermute | solution.py:24
  5.3 11.6 %collective-permute-start.3 = (s32[1,1,2,16]{3,2,1,0:T(2,128)S(1)}, s32[1,1,2,16]{3,2,1,0:T(2,128)S(1)}, u32[]{:S(2)}, u32[]{:S(2)}) collective-permute-start(s32[1,1,2,16]{3,2,1,0:T(2,128)S(1)} %get-tuple-element.15), channel_id=1, source_target_pairs={{0,8},{2,10},{4,12},{6,14},{8,0},{10,2},{12,4},{14,6},{16,24},{18,... | collective-permute-start | bytes 392 | tf_op jit(solution)/shard_map/ppermute | solution.py:24
  7.3 10.8 %collective-permute-start.4 = (s32[1,1,2,16]{3,2,1,0:T(2,128)S(1)}, s32[1,1,2,16]{3,2,1,0:T(2,128)S(1)}, u32[]{:S(2)}, u32[]{:S(2)}) collective-permute-start(s32[1,1,2,16]{3,2,1,0:T(2,128)S(1)} %get-tuple-element.14), channel_id=1, source_target_pairs={{0,10},{2,8},{4,14},{6,12},{8,2},{10,0},{12,6},{14,4},{16,26},{18,... | collective-permute-start | bytes 392 | tf_op jit(solution)/shard_map/ppermute | solution.py:24
  8.7 0.7 %copy-start.1 = (s32[1,16,2]{1,2,0:T(2,128)S(1)}, s32[1,16,2]{1,2,0:T(2,128)}, u32[]{:S(2)}) copy-start(s32[1,16,2]{1,2,0:T(2,128)} %param.6) | copy-start | bytes 388
  11.4 10.4 %collective-permute-start.5 = (s32[1,1,2,16]{3,2,1,0:T(2,128)S(1)}, s32[1,1,2,16]{3,2,1,0:T(2,128)S(1)}, u32[]{:S(2)}, u32[]{:S(2)}) collective-permute-start(s32[1,1,2,16]{3,2,1,0:T(2,128)S(1)} %get-tuple-element.13), channel_id=1, source_target_pairs={{0,12},{2,14},{4,8},{6,10},{8,4},{10,6},{12,0},{14,2},{16,28},{18,... | collective-permute-start | bytes 392 | tf_op jit(solution)/shard_map/ppermute | solution.py:24
  13.9 7.9 %collective-permute-start.6 = (s32[1,1,2,16]{3,2,1,0:T(2,128)S(1)}, s32[1,1,2,16]{3,2,1,0:T(2,128)S(1)}, u32[]{:S(2)}, u32[]{:S(2)}) collective-permute-start(s32[1,1,2,16]{3,2,1,0:T(2,128)S(1)} %get-tuple-element.12), channel_id=1, source_target_pairs={{0,14},{2,12},{4,10},{6,8},{8,6},{10,4},{12,2},{14,0},{16,30},{18,... | collective-permute-start | bytes 392 | tf_op jit(solution)/shard_map/ppermute | solution.py:24
  14.0 11.6 %collective-permute-start.7 = (s32[1,1,2,16]{3,2,1,0:T(2,128)S(1)}, s32[1,1,2,16]{3,2,1,0:T(2,128)S(1)}, u32[]{:S(2)}, u32[]{:S(2)}) collective-permute-start(s32[1,1,2,16]{3,2,1,0:T(2,128)S(1)} %get-tuple-element.11), channel_id=1, source_target_pairs={{0,16},{2,18},{4,20},{6,22},{8,24},{10,26},{12,28},{14,30},{16,0},... | collective-permute-start | bytes 392 | tf_op jit(solution)/shard_map/ppermute | solution.py:24
  16.9 9.9 %collective-permute-start.8 = (s32[1,1,2,16]{3,2,1,0:T(2,128)S(1)}, s32[1,1,2,16]{3,2,1,0:T(2,128)S(1)}, u32[]{:S(2)}, u32[]{:S(2)}) collective-permute-start(s32[1,1,2,16]{3,2,1,0:T(2,128)S(1)} %get-tuple-element.10), channel_id=1, source_target_pairs={{0,18},{2,16},{4,22},{6,20},{8,26},{10,24},{12,30},{14,28},{16,2},... | collective-permute-start | bytes 392 | tf_op jit(solution)/shard_map/ppermute | solution.py:24
  18.2 13.2 %collective-permute-start.9 = (s32[1,1,2,16]{3,2,1,0:T(2,128)S(1)}, s32[1,1,2,16]{3,2,1,0:T(2,128)S(1)}, u32[]{:S(2)}, u32[]{:S(2)}) collective-permute-start(s32[1,1,2,16]{3,2,1,0:T(2,128)S(1)} %get-tuple-element.9), channel_id=1, source_target_pairs={{0,20},{2,22},{4,16},{6,18},{8,28},{10,30},{12,24},{14,26},{16,4},... | collective-permute-start | bytes 392 | tf_op jit(solution)/shard_map/ppermute | solution.py:24
  21.7 9.7 %collective-permute-start.10 = (s32[1,1,2,16]{3,2,1,0:T(2,128)S(1)}, s32[1,1,2,16]{3,2,1,0:T(2,128)S(1)}, u32[]{:S(2)}, u32[]{:S(2)}) collective-permute-start(s32[1,1,2,16]{3,2,1,0:T(2,128)S(1)} %get-tuple-element.8), channel_id=1, source_target_pairs={{0,22},{2,20},{4,18},{6,16},{8,30},{10,28},{12,26},{14,24},{16,6},... | collective-permute-start | bytes 392 | tf_op jit(solution)/shard_map/ppermute | solution.py:24
  21.8 9.6 %collective-permute-start.11 = (s32[1,1,2,16]{3,2,1,0:T(2,128)S(1)}, s32[1,1,2,16]{3,2,1,0:T(2,128)S(1)}, u32[]{:S(2)}, u32[]{:S(2)}) collective-permute-start(s32[1,1,2,16]{3,2,1,0:T(2,128)S(1)} %get-tuple-element.7), channel_id=1, source_target_pairs={{0,24},{2,26},{4,28},{6,30},{8,16},{10,18},{12,20},{14,22},{16,8},... | collective-permute-start | bytes 392 | tf_op jit(solution)/shard_map/ppermute | solution.py:24
  25.6 6.3 %collective-permute-start.12 = (s32[1,1,2,16]{3,2,1,0:T(2,128)S(1)}, s32[1,1,2,16]{3,2,1,0:T(2,128)S(1)}, u32[]{:S(2)}, u32[]{:S(2)}) collective-permute-start(s32[1,1,2,16]{3,2,1,0:T(2,128)S(1)} %get-tuple-element.6), channel_id=1, source_target_pairs={{0,26},{2,24},{4,30},{6,28},{8,18},{10,16},{12,22},{14,20},{16,10}... | collective-permute-start | bytes 392 | tf_op jit(solution)/shard_map/ppermute | solution.py:24
  26.8 6.3 %collective-permute-start.13 = (s32[1,1,2,16]{3,2,1,0:T(2,128)S(1)}, s32[1,1,2,16]{3,2,1,0:T(2,128)S(1)}, u32[]{:S(2)}, u32[]{:S(2)}) collective-permute-start(s32[1,1,2,16]{3,2,1,0:T(2,128)S(1)} %get-tuple-element.19), channel_id=1, source_target_pairs={{0,28},{2,30},{4,24},{6,26},{8,20},{10,22},{12,16},{14,18},{16,12}... | collective-permute-start | bytes 392 | tf_op jit(solution)/shard_map/ppermute | solution.py:24
  31.3 7.2 %collective-permute-start.14 = (s32[1,1,2,16]{3,2,1,0:T(2,128)S(1)}, s32[1,1,2,16]{3,2,1,0:T(2,128)S(1)}, u32[]{:S(2)}, u32[]{:S(2)}) collective-permute-start(s32[1,1,2,16]{3,2,1,0:T(2,128)S(1)} %get-tuple-element.5), channel_id=1, source_target_pairs={{0,30},{2,28},{4,26},{6,24},{8,22},{10,20},{12,18},{14,16},{16,14}... | collective-permute-start | bytes 392 | tf_op jit(solution)/shard_map/ppermute | solution.py:24
  42.9 3.7 %copy-start.2 = (s32[256]{0:T(256)S(1)}, s32[256]{0:T(256)}, u32[]{:S(2)}) copy-start(s32[256]{0:T(256)} %param.7) | copy-start | bytes 3076
  42.9 14.1 %all-to-all-start.1 = ((f32[1,16,2,16,128]{4,3,2,0,1:T(8,128)}), f32[1,16,2,16,128]{4,3,2,0,1:T(8,128)S(1)}, u32[]{:S(2)}, u32[]{:S(2)}) async-start(f32[1,16,2,16,128]{4,3,2,0,1:T(8,128)} %bitcast_multiply_fusion), calls=%async_computation.1 | async-start | bytes 524288 | tf_op jit(solution)/shard_map/all_to_all | solution.py:39
